TPU v7x, 32 devices: a whole 2x2x4 slice. The times are simulated.
32 devices in a mesh: surf: 8 (over y, x, core), probe: 4 (over z).
Axes of the slice: x: 2, y: 2, z: 4, core: 2. Of those that a mesh axis runs over, the one named last changes fastest.
Arguments:
- probes: bfloat16 [32, 65536], P('probe', 'surf'), may hold values from -6 to 6
- sigma: float32 [65536], P('surf'), may hold values from 0.5 to 2
- prior_patch: bfloat16 [128, 128], replicated, may hold values from -0.5 to 0.5
- owner_map: int32 [1024], P('surf'), may hold values from 0 to 7, as said below
- block_perm: int32 [1024], P('surf'), may hold values from 0 to 127, as said below
- col_counts: int32 [1024], P('surf'), may hold values from 1 to 64
- coef: bfloat16 [1024, 1024], P('surf'), may hold values from 0.5 to 1.5
- obs_weight: bfloat16 [1024, 64], P('surf'), may hold values from 0.25 to 1
- column_op: bfloat16 [1024, 1024], replicated, may hold values from -0.1875 to 0.1875
Outputs:
- hess: float32 [32, 65536], P('probe', 'surf')
- diag_est: float32 [65536], P('surf')
- quad: float32 [32], P('probe')
Inputs may be any that keep to these rules, and one draw needn't show every extreme that they name: `owner_map`: the 128 blocks of each surface device go to 8 different column owners, 16 to each. The pairs (owner_map, block_perm) name every slot of every column owner exactly once; a column owner receives 16 blocks from each of 8 surface devices.
All inputs are finite; a program needn't handle non-finite values.
Results may differ from a plain program's by a relative error of at most 0.005.
Values may be sent and summed in bfloat16 or wider, within the bound.
No kernel may reach another device: no remote copies, remote signals or barrier semaphores. Data moves between devices by JAX's collectives and lax.ppermute only.
A program may use at most 64 MiB of HBM per device.

v0:
```python
import jax
import jax.numpy as jnp
from jax import lax
from jax.sharding import PartitionSpec as P

P_SIZE = 32
BS = 64
PATCH = 128


def column_term(fields, coef_rows, obs_rows, counts, valid, column_op):
    rows, width, cols = fields.shape
    layers = coef_rows.shape[1] // cols
    column = lax.broadcasted_iota(jnp.int32, (rows, cols), 1)
    keep = jnp.where((column < counts[:, None]) & valid[:, None], 1.0, 0.0).astype(jnp.float32)
    coef_full = (
        coef_rows.astype(jnp.float32).reshape(rows, 1, layers, cols) * keep[:, None, None, :]
    )
    lifted = (fields.astype(jnp.float32)[:, :, None, :] * coef_full).astype(jnp.bfloat16)
    state = jnp.dot(
        lifted.reshape(rows * width, layers * cols), column_op, preferred_element_type=jnp.float32
    )
    weighted = (
        state.reshape(rows, width, layers, cols) * obs_rows.astype(jnp.float32)[:, None, None, :]
    ).astype(jnp.bfloat16)
    adjoint = lax.dot_general(
        weighted.reshape(rows * width, layers * cols),
        column_op,
        (((1,), (1,)), ((), ())),
        preferred_element_type=jnp.float32,
    )
    return jnp.sum(adjoint.reshape(rows, width, layers, cols) * coef_full, axis=2)


def body(
    probes, sigma, prior_patch, owner_map, block_perm, col_counts, coef, obs_weight, column_op
):
    width, nodes = probes.shape
    blocks = owner_map.shape[0]
    peers = lax.axis_size("surf")
    depth = max(1, blocks // peers)
    slots_all = peers * depth
    grouped = probes.reshape(width, nodes // PATCH, PATCH)
    mixed = jnp.einsum("pki,ij->pkj", grouped, prior_patch, preferred_element_type=jnp.float32)
    spread = (mixed.reshape(width, nodes) * sigma[None, :]).astype(jnp.bfloat16)
    fields = spread.reshape(width, blocks, BS).transpose(1, 0, 2)
    row_ids = lax.broadcasted_iota(jnp.int32, (blocks, blocks), 0)
    col_ids = lax.broadcasted_iota(jnp.int32, (blocks, blocks), 1)
    same = (owner_map[None, :] == owner_map[:, None]) & (col_ids < row_ids)
    rank = jnp.sum(same.astype(jnp.int32), axis=1)
    position = owner_map * depth + rank
    request = (
        jnp.full((slots_all,), -1, jnp.int32).at[position].set(block_perm).reshape(peers, depth)
    )
    asked = lax.all_to_all(request, "surf", split_axis=0, concat_axis=0, tiled=True)
    wanted = asked >= 0
    safe_asked = jnp.maximum(asked, 0)
    coef_out = jnp.where(wanted[:, :, None], coef[safe_asked], jnp.zeros((), jnp.bfloat16))
    obs_out = jnp.where(wanted[:, :, None], obs_weight[safe_asked], jnp.zeros((), jnp.bfloat16))
    coef_in, obs_in = (
        lax.all_to_all(coef_out, "surf", split_axis=0, concat_axis=0, tiled=True),
        lax.all_to_all(obs_out, "surf", split_axis=0, concat_axis=0, tiled=True),
    )
    coef_rows = coef_in.reshape(slots_all, coef.shape[1])[position]
    obs_rows = obs_in.reshape(slots_all, BS)[position]
    everyone = jnp.ones((blocks,), dtype=bool)
    sens = column_term(fields, coef_rows, obs_rows, col_counts, everyone, column_op)
    sens = sens.transpose(1, 0, 2).reshape(width, nodes)
    scaled = (sens * sigma[None, :]).reshape(width, nodes // PATCH, PATCH)
    back = jnp.einsum(
        "pkj,ij->pki", scaled, prior_patch.astype(jnp.float32), precision=lax.Precision.HIGHEST
    ).reshape(width, nodes)
    values = probes.astype(jnp.float32)
    hess = values + back
    product = values * back
    diag_est = lax.psum(jnp.sum(product, axis=0), "probe") / P_SIZE
    quad = lax.psum(jnp.sum(product, axis=1), "surf")
    return (hess, diag_est, quad)


def solution(mesh):
    in_specs = (
        P("probe", "surf"),
        P("surf"),
        P(),
        P("surf"),
        P("surf"),
        P("surf"),
        P("surf", None),
        P("surf", None),
        P(),
    )
    out_specs = (P("probe", "surf"), P("surf"), P("probe"))
    return jax.shard_map(body, mesh=mesh, in_specs=in_specs, out_specs=out_specs, check_vma=False)
```

profile of v0, /device:TPU:0, one launch (start us, length us, event | category | flops | bytes accessed | tf_op | source)
XLA Modules:
  0.0 75.5 jit_solution(10636901468613469254)
XLA Ops:
  0.6 0.0 copy-start
  0.6 0.0 copy-start.6
  0.7 0.9 %convert_reduce_fusion = s32[128]{0:T(128)S(1)} fusion(s32[128]{0:T(128)} %param.12), kind=kLoop, calls=%fused_computation.21 | loop fusion | flops 81792 | bytes 1024 | tf_op jit(solution)/shard_map/reduce_sum | solution.py:50
  1.6 0.7 compare_select_fusion
  2.2 1.1 %scatter_custom_fusion = s32[128]{0:T(128)S(1)} fusion(s32[128]{0:T(128)S(1)} %compare_select_fusion, s32[128]{0:T(128)} %param.13, s32[]{:T(128)} %constant.8.clone.1), kind=kCustom, calls=%fused_computation.35 | custom fusion | bytes 1024 | tf_op jit(solution)/shard_map/scatter | solution.py:53
  3.3 0.7 all_to_all.12
  4.0 5.2 %all-to-all-start = ((s32[8,1,16]{2,1,0:T(1,128)}), s32[8,1,16]{2,1,0:T(1,128)S(1)}, u32[]{:S(2)}, u32[]{:S(2)}) async-start(s32[8,1,16]{2,1,0:T(1,128)} %bitcast.3), calls=%async_computation | async-start | bytes 8192 | tf_op jit(solution)/shard_map/all_to_all | solution.py:55
  9.2 0.8 %mul.80 = f32[128,64]{1,0:T(8,128)S(1)} reshape(f32[8192]{0:T(1024)} %param.10) | data formatting | bytes 65536 | tf_op jit(solution)/shard_map/mul | solution.py:45
  10.0 1.1 %fusion.3 = f32[8,64,128]{2,1,0:T(8,128)S(1)} fusion(bf16[8,64,128]{2,0,1:T(8,128)(2,1)} %bitcast.61, bf16[128,128]{1,0:T(8,128)(2,1)} %param.11), kind=kOutput, calls=%fused_computation.18 | convolution fusion | flops 16777216 | bytes 425984 | tf_op jit(solution)/shard_map/pki,ij->pkj/dot_general | solution.py:44
  11.1 0.1 reshape.128
  11.3 0.0 copy-done.6
  11.3 0.1 copy.60
  11.5 2.4 %all-to-all-done = s32[8,1,16]{2,1,0:T(1,128)S(1)} async-done(((s32[8,1,16]{2,1,0:T(1,128)}), s32[8,1,16]{2,1,0:T(1,128)S(1)}, u32[]{:S(2)}, u32[]{:S(2)}) %all-to-all-start) | async-done | bytes 544 | tf_op jit(solution)/shard_map/all_to_all | solution.py:55
  13.8 0.1 reshape.136
  13.9 0.7 gather_fusion.2
  14.6 0.1 broadcast_select_fusion.1
  14.7 0.7 reshape.188
  15.4 3.3 %all-to-all-start.2 = ((bf16[8,2,512]{2,1,0:T(2,128)(2,1)}), bf16[8,2,512]{2,1,0:T(2,128)(2,1)S(1)}, u32[]{:S(2)}, u32[]{:S(2)}) async-start(bf16[8,2,512]{2,1,0:T(2,128)(2,1)} %reshape.188), calls=%async_computation.2 | async-start | bytes 32768 | tf_op jit(solution)/shard_map/all_to_all | solution.py:62
  18.8 0.0 copy-done
  18.8 0.0 copy-start.1
  18.8 0.9 %gather_fusion = bf16[128,1024]{1,0:T(8,128)(2,1)S(1)} fusion(bf16[128,1024]{1,0:T(8,128)(2,1)S(1)} %copy-done, s32[1024]{0:T(1024)S(1)} %pad_clamp_fusion.1), kind=kCustom, calls=%fused_computation | custom fusion | bytes 524800 | tf_op jit(solution)/shard_map/gather | solution.py:58
  19.7 0.8 %broadcast_select_fusion = bf16[8,16,1024]{2,1,0:T(8,128)(2,1)} fusion(bf16[8,16,1024]{2,1,0:T(8,128)(2,1)S(1)} %bitcast.60, pred[8,16]{1,0:T(8,128)(4,1)S(1)} %compare_bitcast_fusion), kind=kLoop, calls=%fused_computation.15 | loop fusion | flops 131072 | bytes 524416 | tf_op jit(solution)/shard_map/jit(_where)/select_n | solution.py:58
  20.5 3.0 %all-to-all-done.2 = bf16[8,2,512]{2,1,0:T(2,128)(2,1)S(1)} async-done(((bf16[8,2,512]{2,1,0:T(2,128)(2,1)}), bf16[8,2,512]{2,1,0:T(2,128)(2,1)S(1)}, u32[]{:S(2)}, u32[]{:S(2)}) %all-to-all-start.2) | async-done | bytes 16416 | tf_op jit(solution)/shard_map/all_to_all | solution.py:62
  23.5 3.4 %all-to-all-start.1 = ((bf16[8,16,1024]{2,1,0:T(8,128)(2,1)}), bf16[8,16,1024]{2,1,0:T(8,128)(2,1)S(1)}, u32[]{:S(2)}, u32[]{:S(2)}) async-start(bf16[8,16,1024]{2,1,0:T(8,128)(2,1)} %broadcast_select_fusion), calls=%async_computation.1 | async-start | bytes 524288 | tf_op jit(solution)/shard_map/all_to_all | solution.py:61
  26.9 0.9 %copy.53 = f32[128,8,64]{0,2,1:T(8,128)} copy(f32[128,8,64]{2,0,1:T(8,128)S(1)} %convert_bitcast_fusion) | data formatting | bytes 524288 | tf_op jit(solution)/shard_map/convert_element_type | solution.py:19
  27.8 0.0 copy-done.1
  27.8 0.0 copy-start.7
  27.8 2.6 %copy.58 = bf16[1024,1024]{0,1:T(8,128)(2,1)} copy(bf16[1024,1024]{1,0:T(8,128)(2,1)S(1)} %copy-done.1) | data formatting | bytes 4194304 | tf_op args[8]
  30.4 0.0 copy-done.7
  30.4 0.1 reshape.189
  30.5 0.7 gather_fusion.3
  31.2 0.1 copy.61
  31.3 2.4 %all-to-all-done.1 = bf16[8,16,1024]{2,1,0:T(8,128)(2,1)S(1)} async-done(((bf16[8,16,1024]{2,1,0:T(8,128)(2,1)}), bf16[8,16,1024]{2,1,0:T(8,128)(2,1)S(1)}, u32[]{:S(2)}, u32[]{:S(2)}) %all-to-all-start.1) | async-done | bytes 262176 | tf_op jit(solution)/shard_map/all_to_all | solution.py:61
  33.7 0.9 %gather_fusion.1 = bf16[128,1024]{1,0:T(8,128)(2,1)S(1)} fusion(bf16[128,1024]{1,0:T(8,128)(2,1)S(1)} %bitcast.54, s32[1024]{0:T(1024)S(1)} %pad_clamp_fusion), kind=kCustom, calls=%fused_computation.1 | custom fusion | bytes 524800 | tf_op jit(solution)/shard_map/gather | solution.py:64
  34.6 0.1 copy.57
  34.7 0.0 copy-start.2
  34.8 1.7 %multiply_convert_fusion.1 = bf16[128,8,16,64]{0,3,2,1:T(8,128)(2,1)S(1)} fusion(f32[128,16,64]{0,2,1:T(8,128)S(1)} %broadcast_multiply_fusion, f32[128,8,64]{0,2,1:T(8,128)} %copy.53), kind=kLoop, calls=%fused_computation.7 | loop fusion | flops 2097152 | bytes 2883584 | tf_op jit(solution)/shard_map/convert_element_type | solution.py:19
  36.5 0.0 copy-done.2
  36.5 2.4 %multiply_convert_fusion = bf16[128,8,16,64]{0,3,2,1:T(8,128)(2,1)S(1)} fusion(bf16[128,8,1024,1]{0,2,3,1:T(8,128)(2,1)S(1)} %bitcast.58, bf16[16,64,1024,1]{2,1,0,3:T(8,128)(2,1)S(1)} %bitcast.57, f32[128,64]{0,1:T(8,128)S(1)} %convert_element_type.61), kind=kOutput, calls=%fused_computation.6 | convolution fusion | flops 2149580800 | bytes 6324224 | tf_op jit(solution)/shard_map/dot_general | solution.py:20
  38.8 0.0 copy-start.4
  38.9 0.0 copy-start.5
  38.9 2.4 %multiply_reduce_fusion = f32[128,8,64]{0,2,1:T(8,128)S(1)} fusion(bf16[128,8,1024,1]{0,2,3,1:T(8,128)(2,1)S(1)} %bitcast.67, bf16[16,64,1024,1]{2,1,0,3:T(8,128)(2,1)S(1)} %bitcast.56, f32[128,16,64]{0,2,1:T(8,128)S(1)} %broadcast_multiply_fusion), kind=kOutput, calls=%fused_computation.5 | convolution fusion | flops 2149515264 | bytes 4980736 | tf_op jit(solution)/shard_map/dot_general | solution.py:26
  41.3 0.0 copy-start.3
  41.3 0.2 copy.63
  41.5 0.1 reshape.131
  41.6 0.0 copy-done.4
  41.6 0.0 copy-done.5
  41.6 0.3 convolution_bitcast_fusion
  41.9 0.2 copy-done.3
  42.2 1.0 %fusion.1 = (f32[8]{0:T(128)S(1)}, f32[8192]{0:T(1024)S(1)}, f32[8,8192]{1,0:T(8,128)}) fusion(f32[1,8,64,128]{3,2,1,0:T(8,128)S(1)} %convolution_bitcast_fusion, bf16[8,8192]{1,0:T(8,128)(2,1)S(1)} %copy-done.3), kind=kLoop, calls=%fused_computation.16 | loop fusion | flops 319480 | bytes 688160 | tf_op jit(solution)/shard_map/reduce_sum | solution.py:77
  43.2 12.4 %psum.15 = f32[8]{0:T(128)} all-reduce(f32[8]{0:T(128)S(1)} %get-tuple-element.3), channel_id=1, replica_groups=mesh['surf'=8,'probe'=4] {'surf'}, use_global_device_ids=true, to_apply=%region_6.7 | all-reduce | flops 8 | bytes 64 | tf_op jit(solution)/shard_map/psum | solution.py:77
  55.6 19.3 %psum.14 = f32[8192]{0:T(1024)S(1)} all-reduce(f32[8192]{0:T(1024)S(1)} %get-tuple-element.4), channel_id=1, replica_groups=mesh['surf'=8,'probe'=4] {'probe'}, use_global_device_ids=true, to_apply=%region_4.5 | all-reduce | flops 8192 | bytes 65536 | tf_op jit(solution)/shard_map/psum | solution.py:76
  74.9 0.6 broadcast_multiply_fusion.1
  (8 shorter events, 0.1 us)
Async XLA Ops:
  0.6 18.2 %copy-start = (bf16[128,1024]{1,0:T(8,128)(2,1)S(1)}, bf16[128,1024]{1,0:T(8,128)(2,1)}, u32[]{:S(2)}) copy-start(bf16[128,1024]{1,0:T(8,128)(2,1)} %param.15) | copy-start | bytes 786436
  0.6 10.7 %copy-start.6 = (bf16[128,64]{0,1:T(8,128)(2,1)S(1)}, bf16[128,64]{0,1:T(8,128)(2,1)}, u32[]{:S(2)}) copy-start(bf16[128,64]{0,1:T(8,128)(2,1)} %param.16) | copy-start | bytes 49156
  4.0 9.8 %all-to-all-start = ((s32[8,1,16]{2,1,0:T(1,128)}), s32[8,1,16]{2,1,0:T(1,128)S(1)}, u32[]{:S(2)}, u32[]{:S(2)}) async-start(s32[8,1,16]{2,1,0:T(1,128)} %bitcast.3), calls=%async_computation | async-start | bytes 8192 | tf_op jit(solution)/shard_map/all_to_all | solution.py:55
  15.4 8.0 %all-to-all-start.2 = ((bf16[8,2,512]{2,1,0:T(2,128)(2,1)}), bf16[8,2,512]{2,1,0:T(2,128)(2,1)S(1)}, u32[]{:S(2)}, u32[]{:S(2)}) async-start(bf16[8,2,512]{2,1,0:T(2,128)(2,1)} %reshape.188), calls=%async_computation.2 | async-start | bytes 32768 | tf_op jit(solution)/shard_map/all_to_all | solution.py:62
  18.8 9.0 %copy-start.1 = (bf16[1024,1024]{1,0:T(8,128)(2,1)S(1)}, bf16[1024,1024]{1,0:T(8,128)(2,1)}, u32[]{:S(2)}) copy-start(bf16[1024,1024]{1,0:T(8,128)(2,1)} %param.17) | copy-start | bytes 6291460
  23.5 10.3 %all-to-all-start.1 = ((bf16[8,16,1024]{2,1,0:T(8,128)(2,1)}), bf16[8,16,1024]{2,1,0:T(8,128)(2,1)S(1)}, u32[]{:S(2)}, u32[]{:S(2)}) async-start(bf16[8,16,1024]{2,1,0:T(8,128)(2,1)} %broadcast_select_fusion), calls=%async_computation.1 | async-start | bytes 524288 | tf_op jit(solution)/shard_map/all_to_all | solution.py:61
  27.8 2.6 %copy-start.7 = (s32[128]{0:T(128)S(1)}, s32[128]{0:T(128)}, u32[]{:S(2)}) copy-start(s32[128]{0:T(128)} %param.14) | copy-start | bytes 1540
  34.7 1.7 %copy-start.2 = (bf16[1024,1024]{0,1:T(8,128)(2,1)S(1)}, bf16[1024,1024]{0,1:T(8,128)(2,1)}, u32[]{:S(2)}) copy-start(bf16[1024,1024]{0,1:T(8,128)(2,1)} %copy.58) | copy-start | bytes 6291460
  38.8 2.8 %copy-start.4 = (f32[8192]{0:T(1024)S(1)}, f32[8192]{0:T(1024)}, u32[]{:S(2)}) copy-start(f32[8192]{0:T(1024)} %param.10) | copy-start | bytes 98308
  38.9 2.8 %copy-start.5 = (bf16[128,128]{1,0:T(8,128)(2,1)S(1)}, bf16[128,128]{1,0:T(8,128)(2,1)}, u32[]{:S(2)}) copy-start(bf16[128,128]{1,0:T(8,128)(2,1)} %param.11) | copy-start | bytes 98308
  41.3 0.9 %copy-start.3 = (bf16[8,8192]{1,0:T(8,128)(2,1)S(1)}, bf16[8,8192]{1,0:T(8,128)(2,1)}, u32[]{:S(2)}) copy-start(bf16[8,8192]{1,0:T(8,128)(2,1)} %param.9) | copy-start | bytes 393220
where the time goes:
time: 76.1 us; the launch traced here: 75.5 us
  blocking collectives  31.8 us (42%)
  starting transfers between devices  11.9 us (16%)
  local copies, waits for them, and re-layouts  11.2 us (15%)
  waiting for transfers between devices  7.81 us (10%)
  matrix products  6.1 us (8%)
  other arithmetic  5.83 us (8%)
  between operations  0.9 us (1%)
    psum x1, blocking collectives, body(): diag_est = lax.psum(jnp.sum(product, axis=0), 'probe') / P_SIZE  19.3 us
    psum x1, blocking collectives, body(): quad = lax.psum(jnp.sum(product, axis=1), 'surf')  12.4 us
    all_to_all x1, starting transfers between devices, body(): lax.all_to_all(request, 'surf', split_axis=0, concat_axis=0, tiled=True)  5.2 us
    unnamed x20, local copies, waits for them, and re-layouts  3.75 us
    all_to_all x1, starting transfers between devices, body(): lax.all_to_all(coef_out, 'surf', split_axis=0, concat_axis=0, tiled=True)  3.41 us
    all_to_all x1, starting transfers between devices, body(): lax.all_to_all(obs_out, 'surf', split_axis=0, concat_axis=0, tiled=True)  3.34 us
    all_to_all x1, waiting for transfers between devices, body(): lax.all_to_all(obs_out, 'surf', split_axis=0, concat_axis=0, tiled=True)  3.01 us
    all_to_all x1, waiting for transfers between devices, body(): lax.all_to_all(coef_out, 'surf', split_axis=0, concat_axis=0, tiled=True)  2.43 us
  transfers between devices with their start and end apart: 3, of which 3 were waited for; matrix products, arithmetic and copies ran while one was open for 11% of the time, Pallas kernels for 0%

commit v1 on v0

--- a/solution.py
+++ b/solution.py
@@ -2,6 +2,7 @@
 import jax.numpy as jnp
 from jax import lax
 from jax.sharding import PartitionSpec as P
+from jax.lax import all_gather
 
 P_SIZE = 32
 BS = 64
@@ -73,7 +74,8 @@
     values = probes.astype(jnp.float32)
     hess = values + back
     product = values * back
-    diag_est = lax.psum(jnp.sum(product, axis=0), "probe") / P_SIZE
+    fill_cycles = lambda in_array: all_gather(in_array, "probe").sum(axis=0)
+    diag_est = fill_cycles(jnp.sum(product, axis=0)) / P_SIZE
     quad = lax.psum(jnp.sum(product, axis=1), "surf")
     return (hess, diag_est, quad)
 

time: 76.1 us -> 70.5 us (0.926)
  blocking collectives: 31.8 us -> 26 us
    psum x1 -> x0, blocking collectives: 19.3 us -> none  [body(): diag_est = lax.psum(jnp.sum(product, axis=0), 'probe') / P_SIZE]
    all_gather x0 -> x1, blocking collectives: none -> 13.6 us  [body(): fill_cycles = lambda in_array: all_gather(in_array, 'probe').sum(axis=0)]
  transfers between devices with their start and end apart: 3 -> 3, of which waited for: 3 -> 3; matrix products, arithmetic and copies ran while one was open for 11% -> 12% of each run, Pallas kernels for 0% -> 0%
where the time goes in v1:
time: 70.5 us; the launch traced here: 69.9 us
  blocking collectives  26 us (37%)
  starting transfers between devices  11.9 us (17%)
  local copies, waits for them, and re-layouts  11.2 us (16%)
  waiting for transfers between devices  7.81 us (11%)
  matrix products  6.1 us (9%)
  other arithmetic  5.9 us (8%)
  between operations  0.91 us (1%)
    all_gather x1, blocking collectives, body(): fill_cycles = lambda in_array: all_gather(in_array, 'probe').sum(axis=0)  13.6 us
    psum x1, blocking collectives, body(): quad = lax.psum(jnp.sum(product, axis=1), 'surf')  12.4 us
    all_to_all x1, starting transfers between devices, body(): lax.all_to_all(request, 'surf', split_axis=0, concat_axis=0, tiled=True)  5.2 us
    unnamed x20, local copies, waits for them, and re-layouts  3.75 us
    all_to_all x1, starting transfers between devices, body(): lax.all_to_all(coef_out, 'surf', split_axis=0, concat_axis=0, tiled=True)  3.41 us
    all_to_all x1, starting transfers between devices, body(): lax.all_to_all(obs_out, 'surf', split_axis=0, concat_axis=0, tiled=True)  3.34 us
    all_to_all x1, waiting for transfers between devices, body(): lax.all_to_all(obs_out, 'surf', split_axis=0, concat_axis=0, tiled=True)  3.01 us
    all_to_all x1, waiting for transfers between devices, body(): lax.all_to_all(coef_out, 'surf', split_axis=0, concat_axis=0, tiled=True)  2.43 us
  transfers between devices with their start and end apart: 3, of which 3 were waited for; matrix products, arithmetic and copies ran while one was open for 12% of the time, Pallas kernels for 0%

profile of v1, /device:TPU:0, one launch (start us, length us, event | category | flops | bytes accessed | tf_op | source)
XLA Modules:
  0.0 69.9 jit_solution(12286706464674138792)
XLA Ops:
  0.6 0.0 copy-start
  0.6 0.0 copy-start.6
  0.7 0.9 %convert_reduce_fusion = s32[128]{0:T(128)S(1)} fusion(s32[128]{0:T(128)} %param.12), kind=kLoop, calls=%fused_computation.21 | loop fusion | flops 81792 | bytes 1024 | tf_op jit(solution)/shard_map/reduce_sum | solution.py:51
  1.6 0.7 compare_select_fusion
  2.2 1.1 %scatter_custom_fusion = s32[128]{0:T(128)S(1)} fusion(s32[128]{0:T(128)S(1)} %compare_select_fusion, s32[128]{0:T(128)} %param.13, s32[]{:T(128)} %constant.8.clone.1), kind=kCustom, calls=%fused_computation.35 | custom fusion | bytes 1024 | tf_op jit(solution)/shard_map/scatter | solution.py:54
  3.3 0.7 all_to_all.12
  4.0 5.2 %all-to-all-start = ((s32[8,1,16]{2,1,0:T(1,128)}), s32[8,1,16]{2,1,0:T(1,128)S(1)}, u32[]{:S(2)}, u32[]{:S(2)}) async-start(s32[8,1,16]{2,1,0:T(1,128)} %bitcast.3), calls=%async_computation | async-start | bytes 8192 | tf_op jit(solution)/shard_map/all_to_all | solution.py:56
  9.2 0.8 %mul.80 = f32[128,64]{1,0:T(8,128)S(1)} reshape(f32[8192]{0:T(1024)} %param.10) | data formatting | bytes 65536 | tf_op jit(solution)/shard_map/mul | solution.py:46
  10.0 1.1 %fusion.3 = f32[8,64,128]{2,1,0:T(8,128)S(1)} fusion(bf16[8,64,128]{2,0,1:T(8,128)(2,1)} %bitcast.61, bf16[128,128]{1,0:T(8,128)(2,1)} %param.11), kind=kOutput, calls=%fused_computation.18 | convolution fusion | flops 16777216 | bytes 425984 | tf_op jit(solution)/shard_map/pki,ij->pkj/dot_general | solution.py:45
  11.1 0.1 reshape.128
  11.3 0.0 copy-done.6
  11.3 0.1 copy.60
  11.5 2.4 %all-to-all-done = s32[8,1,16]{2,1,0:T(1,128)S(1)} async-done(((s32[8,1,16]{2,1,0:T(1,128)}), s32[8,1,16]{2,1,0:T(1,128)S(1)}, u32[]{:S(2)}, u32[]{:S(2)}) %all-to-all-start) | async-done | bytes 544 | tf_op jit(solution)/shard_map/all_to_all | solution.py:56
  13.8 0.1 reshape.136
  13.9 0.7 %gather_fusion.2 = bf16[128,64]{1,0:T(8,128)(2,1)S(1)} fusion(bf16[128,64]{1,0:T(8,128)(2,1)S(1)} %copy.60, s32[1024]{0:T(1024)S(1)} %pad_clamp_fusion.1), kind=kCustom, calls=%fused_computation.2 | custom fusion | bytes 33280 | tf_op jit(solution)/shard_map/gather | solution.py:60
  14.6 0.1 broadcast_select_fusion.1
  14.7 0.7 %reshape.189 = bf16[8,2,512]{2,1,0:T(2,128)(2,1)} reshape(bf16[8,16,64]{2,1,0:T(8,128)(2,1)S(1)} %broadcast_select_fusion.1) | data formatting | bytes 32768
  15.4 3.3 %all-to-all-start.2 = ((bf16[8,2,512]{2,1,0:T(2,128)(2,1)}), bf16[8,2,512]{2,1,0:T(2,128)(2,1)S(1)}, u32[]{:S(2)}, u32[]{:S(2)}) async-start(bf16[8,2,512]{2,1,0:T(2,128)(2,1)} %reshape.189), calls=%async_computation.2 | async-start | bytes 32768 | tf_op jit(solution)/shard_map/all_to_all | solution.py:63
  18.8 0.0 copy-done
  18.8 0.0 copy-start.1
  18.8 0.9 %gather_fusion = bf16[128,1024]{1,0:T(8,128)(2,1)S(1)} fusion(bf16[128,1024]{1,0:T(8,128)(2,1)S(1)} %copy-done, s32[1024]{0:T(1024)S(1)} %pad_clamp_fusion.1), kind=kCustom, calls=%fused_computation | custom fusion | bytes 524800 | tf_op jit(solution)/shard_map/gather | solution.py:59
  19.7 0.8 %broadcast_select_fusion = bf16[8,16,1024]{2,1,0:T(8,128)(2,1)} fusion(bf16[8,16,1024]{2,1,0:T(8,128)(2,1)S(1)} %bitcast.60, pred[8,16]{1,0:T(8,128)(4,1)S(1)} %compare_bitcast_fusion), kind=kLoop, calls=%fused_computation.15 | loop fusion | flops 131072 | bytes 524416 | tf_op jit(solution)/shard_map/jit(_where)/select_n | solution.py:59
  20.5 3.0 %all-to-all-done.2 = bf16[8,2,512]{2,1,0:T(2,128)(2,1)S(1)} async-done(((bf16[8,2,512]{2,1,0:T(2,128)(2,1)}), bf16[8,2,512]{2,1,0:T(2,128)(2,1)S(1)}, u32[]{:S(2)}, u32[]{:S(2)}) %all-to-all-start.2) | async-done | bytes 16416 | tf_op jit(solution)/shard_map/all_to_all | solution.py:63
  23.5 3.4 %all-to-all-start.1 = ((bf16[8,16,1024]{2,1,0:T(8,128)(2,1)}), bf16[8,16,1024]{2,1,0:T(8,128)(2,1)S(1)}, u32[]{:S(2)}, u32[]{:S(2)}) async-start(bf16[8,16,1024]{2,1,0:T(8,128)(2,1)} %broadcast_select_fusion), calls=%async_computation.1 | async-start | bytes 524288 | tf_op jit(solution)/shard_map/all_to_all | solution.py:62
  26.9 0.9 %copy.53 = f32[128,8,64]{0,2,1:T(8,128)} copy(f32[128,8,64]{2,0,1:T(8,128)S(1)} %convert_bitcast_fusion) | data formatting | bytes 524288 | tf_op jit(solution)/shard_map/convert_element_type | solution.py:20
  27.8 0.0 copy-done.1
  27.8 0.0 copy-start.7
  27.8 2.6 %copy.58 = bf16[1024,1024]{0,1:T(8,128)(2,1)} copy(bf16[1024,1024]{1,0:T(8,128)(2,1)S(1)} %copy-done.1) | data formatting | bytes 4194304 | tf_op args[8]
  30.4 0.0 copy-done.7
  30.4 0.1 reshape.190
  30.5 0.7 %gather_fusion.3 = bf16[128,64]{1,0:T(8,128)(2,1)S(1)} fusion(bf16[128,64]{1,0:T(8,128)(2,1)S(1)} %bitcast.55, s32[1024]{0:T(1024)S(1)} %pad_clamp_fusion), kind=kCustom, calls=%fused_computation.3 | custom fusion | bytes 33280 | tf_op jit(solution)/shard_map/gather | solution.py:66
  31.2 0.1 copy.61
  31.3 2.4 %all-to-all-done.1 = bf16[8,16,1024]{2,1,0:T(8,128)(2,1)S(1)} async-done(((bf16[8,16,1024]{2,1,0:T(8,128)(2,1)}), bf16[8,16,1024]{2,1,0:T(8,128)(2,1)S(1)}, u32[]{:S(2)}, u32[]{:S(2)}) %all-to-all-start.1) | async-done | bytes 262176 | tf_op jit(solution)/shard_map/all_to_all | solution.py:62
  33.7 0.9 %gather_fusion.1 = bf16[128,1024]{1,0:T(8,128)(2,1)S(1)} fusion(bf16[128,1024]{1,0:T(8,128)(2,1)S(1)} %bitcast.54, s32[1024]{0:T(1024)S(1)} %pad_clamp_fusion), kind=kCustom, calls=%fused_computation.1 | custom fusion | bytes 524800 | tf_op jit(solution)/shard_map/gather | solution.py:65
  34.6 0.1 copy.57
  34.7 0.0 copy-start.2
  34.8 1.7 %multiply_convert_fusion.1 = bf16[128,8,16,64]{0,3,2,1:T(8,128)(2,1)S(1)} fusion(f32[128,16,64]{0,2,1:T(8,128)S(1)} %broadcast_multiply_fusion, f32[128,8,64]{0,2,1:T(8,128)} %copy.53), kind=kLoop, calls=%fused_computation.7 | loop fusion | flops 2097152 | bytes 2883584 | tf_op jit(solution)/shard_map/convert_element_type | solution.py:20
  36.5 0.0 copy-done.2
  36.5 2.4 %multiply_convert_fusion = bf16[128,8,16,64]{0,3,2,1:T(8,128)(2,1)S(1)} fusion(bf16[128,8,1024,1]{0,2,3,1:T(8,128)(2,1)S(1)} %bitcast.58, bf16[16,64,1024,1]{2,1,0,3:T(8,128)(2,1)S(1)} %bitcast.57, f32[128,64]{0,1:T(8,128)S(1)} %convert_element_type.61), kind=kOutput, calls=%fused_computation.6 | convolution fusion | flops 2149580800 | bytes 6324224 | tf_op jit(solution)/shard_map/dot_general | solution.py:21
  38.8 0.0 copy-start.4
  38.9 0.0 copy-start.5
  38.9 2.4 %multiply_reduce_fusion = f32[128,8,64]{0,2,1:T(8,128)S(1)} fusion(bf16[128,8,1024,1]{0,2,3,1:T(8,128)(2,1)S(1)} %bitcast.67, bf16[16,64,1024,1]{2,1,0,3:T(8,128)(2,1)S(1)} %bitcast.56, f32[128,16,64]{0,2,1:T(8,128)S(1)} %broadcast_multiply_fusion), kind=kOutput, calls=%fused_computation.5 | convolution fusion | flops 2149515264 | bytes 4980736 | tf_op jit(solution)/shard_map/dot_general | solution.py:27
  41.3 0.0 copy-start.3
  41.3 0.2 copy.63
  41.5 0.1 reshape.131
  41.6 0.0 copy-done.4
  41.6 0.0 copy-done.5
  41.6 0.3 convolution_bitcast_fusion
  41.9 0.2 copy-done.3
  42.2 1.0 %fusion.1 = (f32[8]{0:T(128)S(1)}, f32[8192]{0:T(1024)S(1)}, f32[8,8192]{1,0:T(8,128)}) fusion(f32[1,8,64,128]{3,2,1,0:T(8,128)S(1)} %convolution_bitcast_fusion, bf16[8,8192]{1,0:T(8,128)(2,1)S(1)} %copy-done.3), kind=kLoop, calls=%fused_computation.16 | loop fusion | flops 319480 | bytes 688160 | tf_op jit(solution)/shard_map/reduce_sum | solution.py:79
  43.2 12.4 %psum.7 = f32[8]{0:T(128)} all-reduce(f32[8]{0:T(128)S(1)} %get-tuple-element.3), channel_id=1, replica_groups=mesh['surf'=8,'probe'=4] {'surf'}, use_global_device_ids=true, to_apply=%region_6.7 | all-reduce | flops 8 | bytes 64 | tf_op jit(solution)/shard_map/psum | solution.py:79
  55.6 13.6 %all-gather = f32[32768]{0:T(1024)S(1)} all-gather(f32[8192]{0:T(1024)S(1)} %get-tuple-element.4), channel_id=2, replica_groups=mesh['surf'=8,'probe'=4] {'probe'}, dimensions={0}, use_global_device_ids=true | all-gather | bytes 163840 | tf_op jit(solution)/shard_map/all_gather | solution.py:77
  69.2 0.1 reduce_sum.48
  69.3 0.6 broadcast_multiply_fusion.1
  (9 shorter events, 0.2 us)
Async XLA Ops:
  0.6 18.2 %copy-start = (bf16[128,1024]{1,0:T(8,128)(2,1)S(1)}, bf16[128,1024]{1,0:T(8,128)(2,1)}, u32[]{:S(2)}) copy-start(bf16[128,1024]{1,0:T(8,128)(2,1)} %param.15) | copy-start | bytes 786436
  0.6 10.7 %copy-start.6 = (bf16[128,64]{0,1:T(8,128)(2,1)S(1)}, bf16[128,64]{0,1:T(8,128)(2,1)}, u32[]{:S(2)}) copy-start(bf16[128,64]{0,1:T(8,128)(2,1)} %param.16) | copy-start | bytes 49156
  4.0 9.8 %all-to-all-start = ((s32[8,1,16]{2,1,0:T(1,128)}), s32[8,1,16]{2,1,0:T(1,128)S(1)}, u32[]{:S(2)}, u32[]{:S(2)}) async-start(s32[8,1,16]{2,1,0:T(1,128)} %bitcast.3), calls=%async_computation | async-start | bytes 8192 | tf_op jit(solution)/shard_map/all_to_all | solution.py:56
  15.4 8.0 %all-to-all-start.2 = ((bf16[8,2,512]{2,1,0:T(2,128)(2,1)}), bf16[8,2,512]{2,1,0:T(2,128)(2,1)S(1)}, u32[]{:S(2)}, u32[]{:S(2)}) async-start(bf16[8,2,512]{2,1,0:T(2,128)(2,1)} %reshape.189), calls=%async_computation.2 | async-start | bytes 32768 | tf_op jit(solution)/shard_map/all_to_all | solution.py:63
  18.8 9.0 %copy-start.1 = (bf16[1024,1024]{1,0:T(8,128)(2,1)S(1)}, bf16[1024,1024]{1,0:T(8,128)(2,1)}, u32[]{:S(2)}) copy-start(bf16[1024,1024]{1,0:T(8,128)(2,1)} %param.17) | copy-start | bytes 6291460
  23.5 10.3 %all-to-all-start.1 = ((bf16[8,16,1024]{2,1,0:T(8,128)(2,1)}), bf16[8,16,1024]{2,1,0:T(8,128)(2,1)S(1)}, u32[]{:S(2)}, u32[]{:S(2)}) async-start(bf16[8,16,1024]{2,1,0:T(8,128)(2,1)} %broadcast_select_fusion), calls=%async_computation.1 | async-start | bytes 524288 | tf_op jit(solution)/shard_map/all_to_all | solution.py:62
  27.8 2.6 %copy-start.7 = (s32[128]{0:T(128)S(1)}, s32[128]{0:T(128)}, u32[]{:S(2)}) copy-start(s32[128]{0:T(128)} %param.14) | copy-start | bytes 1540
  34.7 1.7 %copy-start.2 = (bf16[1024,1024]{0,1:T(8,128)(2,1)S(1)}, bf16[1024,1024]{0,1:T(8,128)(2,1)}, u32[]{:S(2)}) copy-start(bf16[1024,1024]{0,1:T(8,128)(2,1)} %copy.58) | copy-start | bytes 6291460
  38.8 2.8 %copy-start.4 = (f32[8192]{0:T(1024)S(1)}, f32[8192]{0:T(1024)}, u32[]{:S(2)}) copy-start(f32[8192]{0:T(1024)} %param.10) | copy-start | bytes 98308
  38.9 2.8 %copy-start.5 = (bf16[128,128]{1,0:T(8,128)(2,1)S(1)}, bf16[128,128]{1,0:T(8,128)(2,1)}, u32[]{:S(2)}) copy-start(bf16[128,128]{1,0:T(8,128)(2,1)} %param.11) | copy-start | bytes 98308
  41.3 0.9 %copy-start.3 = (bf16[8,8192]{1,0:T(8,128)(2,1)S(1)}, bf16[8,8192]{1,0:T(8,128)(2,1)}, u32[]{:S(2)}) copy-start(bf16[8,8192]{1,0:T(8,128)(2,1)} %param.9) | copy-start | bytes 393220
